TPU v7x, 32 devices: a whole 2x2x4 slice. The times are simulated.
32 devices in a mesh: nest: 4 (over x, core), py: 2 (over y), px: 4 (over z).
Axes of the slice: x: 2, y: 2, z: 4, core: 2. Of those that a mesh axis runs over, the one named last changes fastest.
Arguments:
- initial_state: float32 [4, 4, 256, 256], P('nest', None, 'px', 'py'), may hold values from -6 to 6
- drive_modes: float32 [3, 4, 64, 64], replicated, may hold values from -6 to 6
- relax_rates: float32 [4, 4], P('nest'), may hold values from 0.2 to 0.9
- nest_offsets: int32 [4, 2], replicated, may hold values from 0 to 170
Outputs:
- final_state: float32 [4, 4, 256, 256], P('nest', None, 'px', 'py')
- final_modes: float32 [4, 4, 64, 64], P('nest')
Inputs may be any that keep to these rules, and one draw needn't show every extreme that they name: `nest_offsets`: row 0 is not read.
All inputs are finite; a program needn't handle non-finite values.
Results may differ from a plain program's by a relative error of at most 0.0001.
Values sent between devices are 32-bit elements; how exact they have to be, the bound alone decides.
A program may use at most 64 MiB of HBM per device.

v0:
```python
import math
import jax
import jax.numpy as jnp
import numpy as np
from jax import lax
from jax.sharding import PartitionSpec as P

RATIO = 3
RATE = 0.2
HI = lax.Precision.HIGH


def basis(cells, modes, refine, fn=np.cos):
    j = np.arange(modes, dtype=np.int64)
    q = 2 * np.arange(cells, dtype=np.int64) + 1
    product = j[None, :] * q[:, None] % (4 * refine * cells)
    weight = np.where(j == 0, 1.0, 2.0) / cells
    return np.sqrt(weight)[None, :] * fn(np.pi * product / (2.0 * refine * cells))


def half_step(table):
    pad = np.pad(table, ((1, 1), (0, 0)))
    return (0.5 - 2 * RATE) * table + RATE * (pad[2:] + pad[:-2])


def powers(table, count):
    out = [table]
    for _ in range(count):
        out.append(half_step(out[-1]))
    return out


def offset_map(cells, modes, offset):
    base = basis(cells, modes, 1)
    even = jnp.asarray(base.T @ basis(cells, modes, RATIO), jnp.float32)
    odd = jnp.asarray(base.T @ basis(cells, modes, RATIO, np.sin), jnp.float32)
    j = jnp.arange(modes, dtype=jnp.int32)
    product = j * (2 * RATIO * offset) % (4 * RATIO * cells)
    angle = jnp.pi * product.astype(jnp.float32) / (2.0 * RATIO * cells)
    return even * jnp.cos(angle)[None, :] - odd * jnp.sin(angle)[None, :]


def exchange(value, axis, dim, width):
    n, length = (lax.axis_size(axis), value.shape[dim])
    up = [(i, i + 1) for i in range(n - 1)]
    down = [(i + 1, i) for i in range(n - 1)]
    before = lax.ppermute(lax.slice_in_dim(value, length - width, length, axis=dim), axis, up)
    after = lax.ppermute(lax.slice_in_dim(value, 0, width, axis=dim), axis, down)
    return jnp.concatenate([before, value, after], axis=dim)


def free_steps(field, total_x, total_y, steps):
    levels, cx, cy = field.shape
    pad = exchange(exchange(field, "py", 2, steps), "px", 1, steps)
    gx = lax.axis_index("px") * cx - steps + jnp.arange(cx + 2 * steps)
    gy = lax.axis_index("py") * cy - steps + jnp.arange(cy + 2 * steps)
    inside = ((gx >= 0) & (gx < total_x))[:, None] & ((gy >= 0) & (gy < total_y))[None, :]
    for s in range(steps):
        mid = pad[:, 1:-1, 1:-1]
        near = pad[:, 2:, 1:-1] + pad[:, :-2, 1:-1] + pad[:, 1:-1, 2:] + pad[:, 1:-1, :-2]
        pad = mid + RATE * (near - 4.0 * mid)
        cut = s + 1
        pad = jnp.where(inside[cut:-cut, cut:-cut][None], pad, 0.0)
    return pad


def body(initial_state, drive_modes, relax_rates, nest_offsets):
    k = lax.axis_index("nest")
    nests = lax.axis_size("nest")
    field = initial_state[0]
    levels, cx, cy = field.shape
    windows, _, m, _ = drive_modes.shape
    nx, ny = (cx * lax.axis_size("px"), cy * lax.axis_size("py"))
    rp, cp = (powers(basis(nx, m, 1), windows), powers(basis(ny, m, 1), windows))
    a = [jnp.asarray(rp[0].T @ t, jnp.float32) for t in rp]
    b = [jnp.asarray(cp[0].T @ t, jnp.float32) for t in cp]
    u_all = jnp.asarray(np.concatenate(rp, 1), jnp.float32)
    v_all = jnp.asarray(np.concatenate(cp, 1), jnp.float32)
    u = lax.dynamic_slice_in_dim(u_all, lax.axis_index("px") * cx, cx, 0)
    v = lax.dynamic_slice_in_dim(v_all, lax.axis_index("py") * cy, cy, 0)
    half = jnp.einsum("lxy,yq->lxq", field, v, precision=HI)
    rows = []
    for w in range(1, windows + 1):
        terms = [math.comb(w, i) * half[:, :, (w - i) * m : (w - i + 1) * m] for i in range(w + 1)]
        rows.append(
            jnp.einsum(
                "xj,lxm->ljm",
                jnp.concatenate([u[:, i * m : (i + 1) * m] for i in range(w + 1)], 0),
                jnp.concatenate(terms, 1),
                precision=HI,
            )
        )
    shares = lax.psum(jnp.stack(rows), ("py", "px"))
    gain = relax_rates[0][:, None, None]
    row_map = offset_map(nx, m, nest_offsets[k, 0])
    col_map = offset_map(ny, m, nest_offsets[k, 1])

    def left(t, x):
        return jnp.einsum("jp,lpq->ljq", t, x, precision=HI)

    def right(x, t):
        return jnp.einsum("ljq,mq->ljm", x, t, precision=HI)

    def spread(d, x):
        out = left(a[d], x) + right(x, b[d])
        for i in range(1, d):
            out = out + math.comb(d, i) * right(left(a[i], x), b[d - i])
        return out

    parent = jnp.zeros_like(drive_modes)
    for stage in range(nests):
        if stage:
            parent = lax.ppermute(coeffs, "nest", [(i, i + 1) for i in range(nests - 1)])
            interp = jnp.einsum("jp,wlpq->wljq", row_map, parent, precision=HI)
            interp = jnp.einsum("wljq,mq->wljm", interp, col_map, precision=HI)
            target = jnp.where(k == 0, drive_modes, interp)
        else:
            target = drive_modes
        changes, kept = ([], [])
        for w in range(windows):
            own = shares[w]
            for e in range(w):
                own = own + spread(w - e, changes[e])
            changes.append(gain * (target[w] - own))
            kept.append(own + changes[-1])
        coeffs = jnp.stack(kept)
    free = free_steps(field, nx, ny, windows)
    zero = jnp.zeros_like(changes[0])
    blocks = [
        jnp.concatenate(
            [
                math.comb(i + j, i) * changes[windows - 1 - i - j] if i + j < windows else zero
                for j in range(windows)
            ],
            2,
        )
        for i in range(windows)
    ]
    mixed = jnp.concatenate(blocks, 1)
    wide = windows * m
    back = jnp.einsum("lpq,yq->lpy", mixed, v[:, :wide], precision=HI)
    final = free + jnp.einsum("xp,lpy->lxy", u[:, :wide], back, precision=HI)
    return (final[None], coeffs[windows - 1][None])


def solution(mesh):
    spec = P("nest", None, "px", "py")
    return jax.shard_map(
        body,
        mesh=mesh,
        in_specs=(spec, P(), P("nest", None), P()),
        out_specs=(spec, P("nest", None, None, None)),
        check_vma=False,
    )
```

profile of v0, /device:TPU:1, one launch (start us, length us, event | category | flops | bytes accessed | tf_op | source)
XLA Modules:
  0.0 132.8 jit_solution(5296330586854888723)
XLA Ops:
  7.2 1.2 convolution_bitcast_fusion.3
  8.6 0.8 copy-done.7
  10.4 0.8 pad_maximum_fusion
  11.2 0.9 copy-done.3
  12.2 4.1 %collective-permute-start = (f32[4,64,3]{2,1,0:T(8,128)S(1)}, f32[4,64,3]{2,1,0:T(8,128)S(1)}, u32[]{:S(2)}, u32[]{:S(2)}) collective-permute-start(f32[4,64,3]{2,1,0:T(8,128)S(1)} %get-tuple-element.23), channel_id=1, source_target_pairs={{0,4},{1,5},{2,6},{3,7},{8,12},{9,13},{10,14},{11,15},{16,20},{17,... | collective-permute-start | bytes 9224 | tf_op jit(solution)/shard_map/ppermute | solution.py:47
  16.3 1.3 collective-permute-start.1
  17.6 0.7 copy-done.9
  18.3 0.6 constant_dynamic-slice_fusion.2
  20.3 4.1 %collective-permute-done.1 = f32[4,64,3]{2,1,0:T(8,128)S(1)} collective-permute-done((f32[4,64,3]{2,1,0:T(8,128)S(1)}, f32[4,64,3]{2,1,0:T(8,128)S(1)}, u32[]{:S(2)}, u32[]{:S(2)}) %collective-permute-start.1) | collective-permute-done | bytes 3104 | tf_op jit(solution)/shard_map/ppermute | solution.py:48
  24.6 3.2 %collective-permute-start.2 = (f32[4,3,134]{2,1,0:T(4,128)S(1)}, f32[4,3,134]{2,1,0:T(4,128)S(1)}, u32[]{:S(2)}, u32[]{:S(2)}) collective-permute-start(f32[4,3,134]{2,1,0:T(4,128)S(1)} %get-tuple-element.10), channel_id=1, source_target_pairs={{0,1},{1,2},{2,3},{4,5},{5,6},{6,7},{8,9},{9,10},{10,11},{12,13},{... | collective-permute-start | bytes 19304 | tf_op jit(solution)/shard_map/ppermute | solution.py:47
  27.8 1.3 collective-permute-start.3
  29.1 54.7 %all-reduce.3.cloned.1.call-done = f32[3,4,64,64]{3,2,1,0:T(8,128)} async-done(((f32[3,4,64,64]{3,2,1,0:T(8,128)}), f32[3,4,64,64]{3,2,1,0:T(8,128)}) %all-reduce.3.cloned.1.call-update) | async-done | bytes 196624 | tf_op jit(solution)/shard_map/psum | solution.py:93
  83.8 1.0 bitcast_multiply_fusion.2
  85.2 0.6 copy-done.2
  86.7 0.5 copy-done.4
  87.7 5.6 %collective-permute-start.4 = (f32[3,4,64,64]{3,2,1,0:T(8,128)S(1)}, f32[3,4,64,64]{3,2,1,0:T(8,128)S(1)}, u32[]{:S(2)}, u32[]{:S(2)}) collective-permute-start(f32[3,4,64,64]{3,2,1,0:T(8,128)S(1)} %pad_maximum_fusion.1), channel_id=1, source_target_pairs={{0,8},{8,16},{16,24},{1,9},{9,17},{17,25},{2,10},{10,18},{18,26},{... | collective-permute-start | bytes 589832 | tf_op jit(solution)/shard_map/ppermute | solution.py:113
  94.0 4.1 %collective-permute-done.4 = f32[3,4,64,64]{3,2,1,0:T(8,128)S(1)} collective-permute-done((f32[3,4,64,64]{3,2,1,0:T(8,128)S(1)}, f32[3,4,64,64]{3,2,1,0:T(8,128)S(1)}, u32[]{:S(2)}, u32[]{:S(2)}) %collective-permute-start.4) | collective-permute-done | bytes 196640 | tf_op jit(solution)/shard_map/ppermute | solution.py:113
  98.0 0.3 convolution_bitcast_fusion.2
  98.4 0.3 convolution_select_fusion.2
  100.7 4.4 %collective-permute-start.5 = (f32[3,4,64,64]{3,2,1,0:T(8,128)S(1)}, f32[3,4,64,64]{3,2,1,0:T(8,128)S(1)}, u32[]{:S(2)}, u32[]{:S(2)}) collective-permute-start(f32[3,4,64,64]{3,2,1,0:T(8,128)S(1)} %pad_maximum_fusion.2), channel_id=1, source_target_pairs={{0,8},{8,16},{16,24},{1,9},{9,17},{17,25},{2,10},{10,18},{18,26},{... | collective-permute-start | bytes 589832 | tf_op jit(solution)/shard_map/ppermute | solution.py:113
  105.1 0.4 fusion.54
  105.5 4.3 %collective-permute-done.5 = f32[3,4,64,64]{3,2,1,0:T(8,128)S(1)} collective-permute-done((f32[3,4,64,64]{3,2,1,0:T(8,128)S(1)}, f32[3,4,64,64]{3,2,1,0:T(8,128)S(1)}, u32[]{:S(2)}, u32[]{:S(2)}) %collective-permute-start.5) | collective-permute-done | bytes 196640 | tf_op jit(solution)/shard_map/ppermute | solution.py:113
  109.8 0.3 convolution_bitcast_fusion.1
  110.2 0.3 convolution_select_fusion.1
  112.6 4.4 %collective-permute-start.6 = (f32[3,4,64,64]{3,2,1,0:T(8,128)S(1)}, f32[3,4,64,64]{3,2,1,0:T(8,128)S(1)}, u32[]{:S(2)}, u32[]{:S(2)}) collective-permute-start(f32[3,4,64,64]{3,2,1,0:T(8,128)S(1)} %pad_maximum_fusion.3), channel_id=1, source_target_pairs={{0,8},{8,16},{16,24},{1,9},{9,17},{17,25},{2,10},{10,18},{18,26},{... | collective-permute-start | bytes 589832 | tf_op jit(solution)/shard_map/ppermute | solution.py:113
  117.0 0.4 fusion.50
  117.3 4.3 %collective-permute-done.6 = f32[3,4,64,64]{3,2,1,0:T(8,128)S(1)} collective-permute-done((f32[3,4,64,64]{3,2,1,0:T(8,128)S(1)}, f32[3,4,64,64]{3,2,1,0:T(8,128)S(1)}, u32[]{:S(2)}, u32[]{:S(2)}) %collective-permute-start.6) | collective-permute-done | bytes 196640 | tf_op jit(solution)/shard_map/ppermute | solution.py:113
  121.7 0.3 convolution_bitcast_fusion
  122.0 0.3 convolution_select_fusion
  123.6 0.9 add_bitcast_fusion
  124.5 0.5 fusion.20
  125.1 0.9 fusion.1
  (75 shorter events, 9.1 us)
Async XLA Ops:
  7.2 76.6 %all-reduce.3.cloned.1.call-start = ((), (), s32[]{:S(2)}) async-start(), calls=%async_computation | async-start | bytes 786432 | tf_op jit(solution)/shard_map/psum | solution.py:93
  8.4 1.0 copy-start.7
  11.2 0.9 copy-start.3
  12.1 71.7 %copy-start.1 = (f32[3,4,64,64]{3,2,1,0:T(8,128)S(1)}, f32[3,4,64,64]{3,2,1,0:T(8,128)}, u32[]{:S(2)}) copy-start(f32[3,4,64,64]{3,2,1,0:T(8,128)} %param.15) | copy-start | bytes 589828
  12.2 8.2 %collective-permute-start = (f32[4,64,3]{2,1,0:T(8,128)S(1)}, f32[4,64,3]{2,1,0:T(8,128)S(1)}, u32[]{:S(2)}, u32[]{:S(2)}) collective-permute-start(f32[4,64,3]{2,1,0:T(8,128)S(1)} %get-tuple-element.23), channel_id=1, source_target_pairs={{0,4},{1,5},{2,6},{3,7},{8,12},{9,13},{10,14},{11,15},{16,20},{17,... | collective-permute-start | bytes 9224 | tf_op jit(solution)/shard_map/ppermute | solution.py:47
  16.3 8.2 %collective-permute-start.1 = (f32[4,64,3]{2,1,0:T(8,128)S(1)}, f32[4,64,3]{2,1,0:T(8,128)S(1)}, u32[]{:S(2)}, u32[]{:S(2)}) collective-permute-start(f32[4,64,3]{2,1,0:T(8,128)S(1)} %get-tuple-element.24), channel_id=1, source_target_pairs={{4,0},{5,1},{6,2},{7,3},{12,8},{13,9},{14,10},{15,11},{20,16},{21,... | collective-permute-start | bytes 9224 | tf_op jit(solution)/shard_map/ppermute | solution.py:48
  17.6 0.7 copy-start.9
  24.6 69.2 %collective-permute-start.2 = (f32[4,3,134]{2,1,0:T(4,128)S(1)}, f32[4,3,134]{2,1,0:T(4,128)S(1)}, u32[]{:S(2)}, u32[]{:S(2)}) collective-permute-start(f32[4,3,134]{2,1,0:T(4,128)S(1)} %get-tuple-element.10), channel_id=1, source_target_pairs={{0,1},{1,2},{2,3},{4,5},{5,6},{6,7},{8,9},{9,10},{10,11},{12,13},{... | collective-permute-start | bytes 19304 | tf_op jit(solution)/shard_map/ppermute | solution.py:47
  27.8 56.0 %copy-start.8 = (f32[1,4]{1,0:T(1,128)S(1)}, f32[1,4]{1,0:T(1,128)}, u32[]{:S(2)}) copy-start(f32[1,4]{1,0:T(1,128)} %param.16) | copy-start | bytes 52
  27.8 65.9 %collective-permute-start.3 = (f32[4,3,134]{2,1,0:T(4,128)S(1)}, f32[4,3,134]{2,1,0:T(4,128)S(1)}, u32[]{:S(2)}, u32[]{:S(2)}) collective-permute-start(f32[4,3,134]{2,1,0:T(4,128)S(1)} %get-tuple-element.11), channel_id=1, source_target_pairs={{1,0},{2,1},{3,2},{5,4},{6,5},{7,6},{9,8},{10,9},{11,10},{13,12},{... | collective-permute-start | bytes 19304 | tf_op jit(solution)/shard_map/ppermute | solution.py:48
  83.8 1.0 copy-start
  84.8 1.0 copy-start.2
  86.4 0.8 copy-start.4
  87.7 10.3 %collective-permute-start.4 = (f32[3,4,64,64]{3,2,1,0:T(8,128)S(1)}, f32[3,4,64,64]{3,2,1,0:T(8,128)S(1)}, u32[]{:S(2)}, u32[]{:S(2)}) collective-permute-start(f32[3,4,64,64]{3,2,1,0:T(8,128)S(1)} %pad_maximum_fusion.1), channel_id=1, source_target_pairs={{0,8},{8,16},{16,24},{1,9},{9,17},{17,25},{2,10},{10,18},{18,26},{... | collective-permute-start | bytes 589832 | tf_op jit(solution)/shard_map/ppermute | solution.py:113
  93.7 4.3 %copy-start.5 = (f32[64,64]{1,0:T(8,128)S(1)}, f32[64,64]{1,0:T(8,128)}, u32[]{:S(2)}) copy-start(f32[64,64]{1,0:T(8,128)} %constant.86.clone) | copy-start | bytes 49156
  93.7 4.3 %copy-start.6 = (f32[64,64]{1,0:T(8,128)S(1)}, f32[64,64]{1,0:T(8,128)}, u32[]{:S(2)}) copy-start(f32[64,64]{1,0:T(8,128)} %constant.87.clone) | copy-start | bytes 49156
  100.7 9.1 %collective-permute-start.5 = (f32[3,4,64,64]{3,2,1,0:T(8,128)S(1)}, f32[3,4,64,64]{3,2,1,0:T(8,128)S(1)}, u32[]{:S(2)}, u32[]{:S(2)}) collective-permute-start(f32[3,4,64,64]{3,2,1,0:T(8,128)S(1)} %pad_maximum_fusion.2), channel_id=1, source_target_pairs={{0,8},{8,16},{16,24},{1,9},{9,17},{17,25},{2,10},{10,18},{18,26},{... | collective-permute-start | bytes 589832 | tf_op jit(solution)/shard_map/ppermute | solution.py:113
  112.6 9.1 %collective-permute-start.6 = (f32[3,4,64,64]{3,2,1,0:T(8,128)S(1)}, f32[3,4,64,64]{3,2,1,0:T(8,128)S(1)}, u32[]{:S(2)}, u32[]{:S(2)}) collective-permute-start(f32[3,4,64,64]{3,2,1,0:T(8,128)S(1)} %pad_maximum_fusion.3), channel_id=1, source_target_pairs={{0,8},{8,16},{16,24},{1,9},{9,17},{17,25},{2,10},{10,18},{18,26},{... | collective-permute-start | bytes 589832 | tf_op jit(solution)/shard_map/ppermute | solution.py:113
Sparse Core Ops, SparseCore 0:
  11.3 72.4 all-reduce.2
where the time goes:
time: 133 us
  waiting for transfers between devices  71.5 us (54%)
  starting transfers between devices  24.4 us (18%)
  between operations  16 us (12%)
  matrix products  12.6 us (9%)
  local copies, waits for them, and re-layouts  4.49 us (3%)
  other arithmetic  3.84 us (3%)
    psum x1, waiting for transfers between devices, body(): shares = lax.psum(jnp.stack(rows), ('py', 'px'))  54.7 us
    ppermute x3, starting transfers between devices, body(): lax.ppermute(coeffs, 'nest', [(i, i + 1) for i in range(nests - 1)])  14.4 us
    ppermute x3, waiting for transfers between devices, body(): lax.ppermute(coeffs, 'nest', [(i, i + 1) for i in range(nests - 1)])  12.7 us
    ppermute x2, starting transfers between devices, exchange(): lax.ppermute(lax.slice_in_dim(value, length - width, length, axis=dim), a...  7.35 us
    dot_general x16, matrix products, right(): return jnp.einsum('ljq,mq->ljm', x, t, precision=HI)  4.38 us
    ppermute x2, waiting for transfers between devices, exchange(): lax.ppermute(lax.slice_in_dim(value, 0, width, axis=dim), axis, down)  4.13 us
    unnamed x20, local copies, waits for them, and re-layouts  3.45 us
    dot_general x12, matrix products, left(): return jnp.einsum('jp,lpq->ljq', t, x, precision=HI)  2.86 us
  transfers between devices with their start and end apart: 8, of which 5 were waited for; matrix products, arithmetic and copies ran while one was open for 4% of the time, Pallas kernels for 0%

commit v1 on v0

--- a/solution.py
+++ b/solution.py
@@ -90,7 +90,9 @@
                 precision=HI,
             )
         )
-    shares = lax.psum(jnp.stack(rows), ("py", "px"))
+    own_2 = jnp.stack(rows)
+    parts = lax.all_gather(own_2, ("py", "px"))
+    shares = jnp.sum(parts, axis=0)
     gain = relax_rates[0][:, None, None]
     row_map = offset_map(nx, m, nest_offsets[k, 0])
     col_map = offset_map(ny, m, nest_offsets[k, 1])

time: 133 us -> 123 us (0.925)
  waiting for transfers between devices: 71.5 us -> 61.8 us
  local copies, waits for them, and re-layouts: 4.49 us -> 2.88 us
    psum x1 -> x0, waiting for transfers between devices: 54.7 us -> none  [body(): shares = lax.psum(jnp.stack(rows), ('py', 'px'))]
    all_gather x0 -> x1, waiting for transfers between devices: none -> 46.7 us  [body(): parts = lax.all_gather(own_2, ('py', 'px'))]
    unnamed x20 -> x18, local copies, waits for them, and re-layouts: 3.45 us -> 0.05 us
    reduce_sum x0 -> x1, other arithmetic: none -> 2.28 us  [body(): shares = jnp.sum(parts, axis=0)]
    ppermute x2, waiting for transfers between devices: 4.13 us -> 2.31 us  [exchange(): lax.ppermute(lax.slice_in_dim(value, 0, width, axis=dim), axis, down)]
  transfers between devices with their start and end apart: 8 -> 8, of which waited for: 5 -> 5; matrix products, arithmetic and copies ran while one was open for 4% -> 5% of each run, Pallas kernels for 0% -> 0%
where the time goes in v1:
time: 123 us; the launch traced here: 122 us
  waiting for transfers between devices  61.8 us (50%)
  starting transfers between devices  24 us (20%)
  between operations  16 us (13%)
  matrix products  13.3 us (11%)
  other arithmetic  4.44 us (4%)
  local copies, waits for them, and re-layouts  2.88 us (2%)
    all_gather x1, waiting for transfers between devices, body(): parts = lax.all_gather(own_2, ('py', 'px'))  46.7 us
    ppermute x3, starting transfers between devices, body(): lax.ppermute(coeffs, 'nest', [(i, i + 1) for i in range(nests - 1)])  14.2 us
    ppermute x3, waiting for transfers between devices, body(): lax.ppermute(coeffs, 'nest', [(i, i + 1) for i in range(nests - 1)])  12.7 us
    ppermute x2, starting transfers between devices, exchange(): lax.ppermute(lax.slice_in_dim(value, length - width, length, axis=dim), a...  7.15 us
    dot_general x16, matrix products, right(): return jnp.einsum('ljq,mq->ljm', x, t, precision=HI)  4.38 us
    dot_general x12, matrix products, left(): return jnp.einsum('jp,lpq->ljq', t, x, precision=HI)  2.86 us
    ppermute x2, starting transfers between devices, exchange(): lax.ppermute(lax.slice_in_dim(value, 0, width, axis=dim), axis, down)  2.58 us
  transfers between devices with their start and end apart: 8, of which 5 were waited for; matrix products, arithmetic and copies ran while one was open for 5% of the time, Pallas kernels for 0%

profile of v1, /device:TPU:1, one launch (start us, length us, event | category | flops | bytes accessed | tf_op | source)
XLA Modules:
  0.0 122.4 jit_solution(1179527973240210395)
XLA Ops:
  7.2 1.3 %convolution_bitcast_fusion.3 = f32[4,64,256]{2,1,0:T(8,128)S(1)} fusion(f32[256,256]{1,0:T(8,128)} %constant.85.clone, s32[]{:T(128)S(6)} %select_n.67, f32[1,4,64,128]{3,2,1,0:T(8,128)} %param.14), kind=kOutput, calls=%fused_computation.6 | convolution fusion | flops 50331648 | bytes 524292 | tf_op jit(solution)/shard_map/lxy,yq->lxq/dot_general | solution.py:81
  8.6 1.0 constant_dynamic-slice_fusion
  9.6 0.4 convolution_bitcast_fusion.19
  10.0 0.5 convolution_bitcast_fusion.6
  10.5 0.6 convolution_bitcast_fusion.5
  11.2 0.9 copy.46
  12.2 4.0 %collective-permute-start = (f32[4,64,3]{2,1,0:T(8,128)S(1)}, f32[4,64,3]{2,1,0:T(8,128)S(1)}, u32[]{:S(2)}, u32[]{:S(2)}) collective-permute-start(f32[4,64,3]{2,1,0:T(8,128)S(1)} %get-tuple-element.23), channel_id=1, source_target_pairs={{0,4},{1,5},{2,6},{3,7},{8,12},{9,13},{10,14},{11,15},{16,20},{17,... | collective-permute-start | bytes 9224 | tf_op jit(solution)/shard_map/ppermute | solution.py:47
  16.2 1.3 %collective-permute-start.1 = (f32[4,64,3]{2,1,0:T(8,128)S(1)}, f32[4,64,3]{2,1,0:T(8,128)S(1)}, u32[]{:S(2)}, u32[]{:S(2)}) collective-permute-start(f32[4,64,3]{2,1,0:T(8,128)S(1)} %get-tuple-element.24), channel_id=1, source_target_pairs={{4,0},{5,1},{6,2},{7,3},{12,8},{13,9},{14,10},{15,11},{20,16},{21,... | collective-permute-start | bytes 9224 | tf_op jit(solution)/shard_map/ppermute | solution.py:48
  17.5 0.6 constant_dynamic-slice_fusion.2
  19.6 2.3 %collective-permute-done.1 = f32[4,64,3]{2,1,0:T(8,128)S(1)} collective-permute-done((f32[4,64,3]{2,1,0:T(8,128)S(1)}, f32[4,64,3]{2,1,0:T(8,128)S(1)}, u32[]{:S(2)}, u32[]{:S(2)}) %collective-permute-start.1) | collective-permute-done | bytes 3104 | tf_op jit(solution)/shard_map/ppermute | solution.py:48
  22.0 3.2 %collective-permute-start.2 = (f32[4,3,134]{2,1,0:T(4,128)S(1)}, f32[4,3,134]{2,1,0:T(4,128)S(1)}, u32[]{:S(2)}, u32[]{:S(2)}) collective-permute-start(f32[4,3,134]{2,1,0:T(4,128)S(1)} %get-tuple-element.10), channel_id=1, source_target_pairs={{0,1},{1,2},{2,3},{4,5},{5,6},{6,7},{8,9},{9,10},{10,11},{12,13},{... | collective-permute-start | bytes 19304 | tf_op jit(solution)/shard_map/ppermute | solution.py:47
  25.2 1.3 %collective-permute-start.3 = (f32[4,3,134]{2,1,0:T(4,128)S(1)}, f32[4,3,134]{2,1,0:T(4,128)S(1)}, u32[]{:S(2)}, u32[]{:S(2)}) collective-permute-start(f32[4,3,134]{2,1,0:T(4,128)S(1)} %get-tuple-element.11), channel_id=1, source_target_pairs={{1,0},{2,1},{3,2},{5,4},{6,5},{7,6},{9,8},{10,9},{11,10},{13,12},{... | collective-permute-start | bytes 19304 | tf_op jit(solution)/shard_map/ppermute | solution.py:48
  26.5 46.7 %all-gather.3.cloned.1.call-done = f32[24,4,64,64]{3,2,1,0:T(8,128)} async-done(((f32[3,4,64,64]{3,2,1,0:T(8,128)}), f32[24,4,64,64]{3,2,1,0:T(8,128)}) %all-gather.3.cloned.1.call-update) | async-done | bytes 1572880 | tf_op jit(solution)/shard_map/all_gather | solution.py:94
  73.2 2.3 %reduce_sum.9 = f32[3,4,64,64]{3,2,1,0:T(8,128)S(1)} reduce(f32[8,3,4,64,64]{4,3,2,1,0:T(8,128)} %bitcast.271, f32[]{:T(128)} %constant.37.clone.1), dimensions={0}, to_apply=%region_0.0 | reduce | flops 344064 | bytes 1769476 | tf_op jit(solution)/shard_map/reduce_sum | solution.py:95
  76.3 0.3 convolution_bitcast_fusion.16
  77.5 5.4 %collective-permute-start.4 = (f32[3,4,64,64]{3,2,1,0:T(8,128)S(1)}, f32[3,4,64,64]{3,2,1,0:T(8,128)S(1)}, u32[]{:S(2)}, u32[]{:S(2)}) collective-permute-start(f32[3,4,64,64]{3,2,1,0:T(8,128)S(1)} %pad_maximum_fusion.1), channel_id=1, source_target_pairs={{0,8},{8,16},{16,24},{1,9},{9,17},{17,25},{2,10},{10,18},{18,26},{... | collective-permute-start | bytes 589832 | tf_op jit(solution)/shard_map/ppermute | solution.py:115
  83.5 4.1 %collective-permute-done.4 = f32[3,4,64,64]{3,2,1,0:T(8,128)S(1)} collective-permute-done((f32[3,4,64,64]{3,2,1,0:T(8,128)S(1)}, f32[3,4,64,64]{3,2,1,0:T(8,128)S(1)}, u32[]{:S(2)}, u32[]{:S(2)}) %collective-permute-start.4) | collective-permute-done | bytes 196640 | tf_op jit(solution)/shard_map/ppermute | solution.py:115
  87.6 0.3 convolution_bitcast_fusion.2
  87.9 0.3 convolution_select_fusion.2
  90.3 4.4 %collective-permute-start.5 = (f32[3,4,64,64]{3,2,1,0:T(8,128)S(1)}, f32[3,4,64,64]{3,2,1,0:T(8,128)S(1)}, u32[]{:S(2)}, u32[]{:S(2)}) collective-permute-start(f32[3,4,64,64]{3,2,1,0:T(8,128)S(1)} %pad_maximum_fusion.2), channel_id=1, source_target_pairs={{0,8},{8,16},{16,24},{1,9},{9,17},{17,25},{2,10},{10,18},{18,26},{... | collective-permute-start | bytes 589832 | tf_op jit(solution)/shard_map/ppermute | solution.py:115
  94.7 0.4 fusion.54
  95.1 4.3 %collective-permute-done.5 = f32[3,4,64,64]{3,2,1,0:T(8,128)S(1)} collective-permute-done((f32[3,4,64,64]{3,2,1,0:T(8,128)S(1)}, f32[3,4,64,64]{3,2,1,0:T(8,128)S(1)}, u32[]{:S(2)}, u32[]{:S(2)}) %collective-permute-start.5) | collective-permute-done | bytes 196640 | tf_op jit(solution)/shard_map/ppermute | solution.py:115
  99.4 0.3 convolution_bitcast_fusion.1
  99.7 0.3 convolution_select_fusion.1
  102.1 4.4 %collective-permute-start.6 = (f32[3,4,64,64]{3,2,1,0:T(8,128)S(1)}, f32[3,4,64,64]{3,2,1,0:T(8,128)S(1)}, u32[]{:S(2)}, u32[]{:S(2)}) collective-permute-start(f32[3,4,64,64]{3,2,1,0:T(8,128)S(1)} %pad_maximum_fusion.3), channel_id=1, source_target_pairs={{0,8},{8,16},{16,24},{1,9},{9,17},{17,25},{2,10},{10,18},{18,26},{... | collective-permute-start | bytes 589832 | tf_op jit(solution)/shard_map/ppermute | solution.py:115
  106.5 0.4 fusion.50
  106.9 4.3 %collective-permute-done.6 = f32[3,4,64,64]{3,2,1,0:T(8,128)S(1)} collective-permute-done((f32[3,4,64,64]{3,2,1,0:T(8,128)S(1)}, f32[3,4,64,64]{3,2,1,0:T(8,128)S(1)}, u32[]{:S(2)}, u32[]{:S(2)}) %collective-permute-start.6) | collective-permute-done | bytes 196640 | tf_op jit(solution)/shard_map/ppermute | solution.py:115
  111.2 0.3 convolution_bitcast_fusion
  111.5 0.3 convolution_select_fusion
  113.2 0.9 add_bitcast_fusion
  114.1 0.5 fusion.20
  114.6 0.9 fusion.1
  (75 shorter events, 8.0 us)
Async XLA Ops:
  7.2 66.0 %all-gather.3.cloned.1.call-start = ((), (), s32[]{:S(2)}) async-start(), calls=%async_computation | async-start | bytes 3538944 | tf_op jit(solution)/shard_map/all_gather | solution.py:94
  7.2 4.9 %copy-start.2 = (f32[1,4,64,128]{3,2,1,0:T(8,128)S(1)}, f32[1,4,64,128]{3,2,1,0:T(8,128)}, u32[]{:S(2)}) copy-start(f32[1,4,64,128]{3,2,1,0:T(8,128)} %param.14) | copy-start | bytes 393220
  8.5 9.0 %copy-start.8 = (s32[4,2]{0,1:T(2,128)S(1)}, s32[4,2]{0,1:T(2,128)}, u32[]{:S(2)}) copy-start(s32[4,2]{0,1:T(2,128)} %param.17) | copy-start | bytes 100
  11.1 64.4 %copy-start.1 = (f32[3,4,64,64]{3,2,1,0:T(8,128)S(1)}, f32[3,4,64,64]{3,2,1,0:T(8,128)}, u32[]{:S(2)}) copy-start(f32[3,4,64,64]{3,2,1,0:T(8,128)} %param.15) | copy-start | bytes 589828
  11.1 64.4 %copy-start.7 = (f32[1,4]{1,0:T(1,128)S(1)}, f32[1,4]{1,0:T(1,128)}, u32[]{:S(2)}) copy-start(f32[1,4]{1,0:T(1,128)} %param.16) | copy-start | bytes 52
  11.2 64.4 %copy-start = (f32[64,64,1]{1,0,2:T(8,128)S(1)}, f32[64,64,1]{1,0,2:T(8,128)}, u32[]{:S(2)}) copy-start(f32[64,64,1]{1,0,2:T(8,128)} %constant.92) | copy-start | bytes 49156
  12.2 7.4 %collective-permute-start = (f32[4,64,3]{2,1,0:T(8,128)S(1)}, f32[4,64,3]{2,1,0:T(8,128)S(1)}, u32[]{:S(2)}, u32[]{:S(2)}) collective-permute-start(f32[4,64,3]{2,1,0:T(8,128)S(1)} %get-tuple-element.23), channel_id=1, source_target_pairs={{0,4},{1,5},{2,6},{3,7},{8,12},{9,13},{10,14},{11,15},{16,20},{17,... | collective-permute-start | bytes 9224 | tf_op jit(solution)/shard_map/ppermute | solution.py:47
  16.2 5.7 %collective-permute-start.1 = (f32[4,64,3]{2,1,0:T(8,128)S(1)}, f32[4,64,3]{2,1,0:T(8,128)S(1)}, u32[]{:S(2)}, u32[]{:S(2)}) collective-permute-start(f32[4,64,3]{2,1,0:T(8,128)S(1)} %get-tuple-element.24), channel_id=1, source_target_pairs={{4,0},{5,1},{6,2},{7,3},{12,8},{13,9},{14,10},{15,11},{20,16},{21,... | collective-permute-start | bytes 9224 | tf_op jit(solution)/shard_map/ppermute | solution.py:48
  22.0 61.3 %collective-permute-start.2 = (f32[4,3,134]{2,1,0:T(4,128)S(1)}, f32[4,3,134]{2,1,0:T(4,128)S(1)}, u32[]{:S(2)}, u32[]{:S(2)}) collective-permute-start(f32[4,3,134]{2,1,0:T(4,128)S(1)} %get-tuple-element.10), channel_id=1, source_target_pairs={{0,1},{1,2},{2,3},{4,5},{5,6},{6,7},{8,9},{9,10},{10,11},{12,13},{... | collective-permute-start | bytes 19304 | tf_op jit(solution)/shard_map/ppermute | solution.py:47
  25.2 58.1 %collective-permute-start.3 = (f32[4,3,134]{2,1,0:T(4,128)S(1)}, f32[4,3,134]{2,1,0:T(4,128)S(1)}, u32[]{:S(2)}, u32[]{:S(2)}) collective-permute-start(f32[4,3,134]{2,1,0:T(4,128)S(1)} %get-tuple-element.11), channel_id=1, source_target_pairs={{1,0},{2,1},{3,2},{5,4},{6,5},{7,6},{9,8},{10,9},{11,10},{13,12},{... | collective-permute-start | bytes 19304 | tf_op jit(solution)/shard_map/ppermute | solution.py:48
  73.2 3.8 %copy-start.3 = (f32[64,64,1]{1,0,2:T(8,128)S(1)}, f32[64,64,1]{1,0,2:T(8,128)}, u32[]{:S(2)}) copy-start(f32[64,64,1]{1,0,2:T(8,128)} %constant.93) | copy-start | bytes 49156
  75.5 12.1 %copy-start.4 = (f32[64,64]{1,0:T(8,128)S(1)}, f32[64,64]{1,0:T(8,128)}, u32[]{:S(2)}) copy-start(f32[64,64]{1,0:T(8,128)} %constant.86.clone) | copy-start | bytes 49156
  75.5 12.1 %copy-start.5 = (f32[64,64]{1,0:T(8,128)S(1)}, f32[64,64]{1,0:T(8,128)}, u32[]{:S(2)}) copy-start(f32[64,64]{1,0:T(8,128)} %constant.87.clone) | copy-start | bytes 49156
  77.5 10.1 %collective-permute-start.4 = (f32[3,4,64,64]{3,2,1,0:T(8,128)S(1)}, f32[3,4,64,64]{3,2,1,0:T(8,128)S(1)}, u32[]{:S(2)}, u32[]{:S(2)}) collective-permute-start(f32[3,4,64,64]{3,2,1,0:T(8,128)S(1)} %pad_maximum_fusion.1), channel_id=1, source_target_pairs={{0,8},{8,16},{16,24},{1,9},{9,17},{17,25},{2,10},{10,18},{18,26},{... | collective-permute-start | bytes 589832 | tf_op jit(solution)/shard_map/ppermute | solution.py:115
  90.3 9.1 %collective-permute-start.5 = (f32[3,4,64,64]{3,2,1,0:T(8,128)S(1)}, f32[3,4,64,64]{3,2,1,0:T(8,128)S(1)}, u32[]{:S(2)}, u32[]{:S(2)}) collective-permute-start(f32[3,4,64,64]{3,2,1,0:T(8,128)S(1)} %pad_maximum_fusion.2), channel_id=1, source_target_pairs={{0,8},{8,16},{16,24},{1,9},{9,17},{17,25},{2,10},{10,18},{18,26},{... | collective-permute-start | bytes 589832 | tf_op jit(solution)/shard_map/ppermute | solution.py:115
  102.1 9.1 %collective-permute-start.6 = (f32[3,4,64,64]{3,2,1,0:T(8,128)S(1)}, f32[3,4,64,64]{3,2,1,0:T(8,128)S(1)}, u32[]{:S(2)}, u32[]{:S(2)}) collective-permute-start(f32[3,4,64,64]{3,2,1,0:T(8,128)S(1)} %pad_maximum_fusion.3), channel_id=1, source_target_pairs={{0,8},{8,16},{16,24},{1,9},{9,17},{17,25},{2,10},{10,18},{18,26},{... | collective-permute-start | bytes 589832 | tf_op jit(solution)/shard_map/ppermute | solution.py:115
  106.9 7.2 %copy-start.6 = (f32[256,256]{1,0:T(8,128)S(1)}, f32[256,256]{1,0:T(8,128)}, u32[]{:S(2)}) copy-start(f32[256,256]{1,0:T(8,128)} %constant.85.clone) | copy-start | bytes 786436
Sparse Core Ops, SparseCore 0:
  12.2 60.9 all-gather.2
